TPU v7x, 256 devices: a whole 4x4x8 slice. The times are simulated.
256 devices in a mesh: space: 4 (over y_hi, core), shard: 64 (over x, z, y_lo).
Axes of the slice: x: 4, y: 4 (y_hi: 2, y_lo: 2; y = y_hi * 2 + y_lo), z: 8, core: 2. Of those that a mesh axis runs over, the one named last changes fastest.
Arguments:
- volume_field: float32 [2, 16, 16, 1024, 128], P(None, None, 'space', 'shard'), may hold values from -6 to 6
- source: float32 [2, 16, 16, 1024, 128], P(None, None, 'space', 'shard'), may hold values from -6 to 6
- material: int32 [16, 1024, 128], P('space', 'shard'), may hold values from 0 to 7
- mat_real: float32 [8], replicated, may hold values from 0.5 to 4
- mat_loss: float32 [8], replicated, may hold values from 0.1 to 1.5
- surface_map: int32 [4096, 128], P(('space', 'shard')), may hold values from 0 to 8191
- near_boxes: int32 [4096, 4], P(('space', 'shard')), may hold values from 0 to 4095, as said below
- near_blocks: bfloat16 [4, 256, 256], replicated, may hold values from -0.1875 to 0.1875
- radiate: bfloat16 [2, 128, 512], replicated, may hold values from -0.375 to 0.375
- interp: bfloat16 [512, 2048], replicated, may hold values from -0.25 to 0.25
- phase_angle: float32 [8, 2048], replicated, may hold values from -3.140625 to 3.140625
- far_parents: int32 [512, 8], replicated, may hold values from 0 to 511
- far_kind: int32 [512, 8], replicated, may hold values from 0 to 315
- translate: float32 [316, 2, 2048], P(None, None, 'shard'), may hold values from -0.18 to 0.18
Outputs:
- volume_out: float32 [2, 16, 16, 1024, 128], P(None, None, 'space', 'shard')
- forcing: float32 [4096, 16, 256], P(('space', 'shard'))
Inputs may be any that keep to these rules, and one draw needn't show every extreme that they name: near_boxes[b, 0] = b; every other entry is a box of the same group of 1024 boxes (boxes g * 1024 to (g + 1) * 1024 - 1) whose index lies from 16 below to 31 above the first box of b's run of 16 boxes.
All inputs are finite; a program needn't handle non-finite values.
Results may differ from a plain program's by a relative error of at most 0.015.
Values may be sent and summed in bfloat16 or wider, within the bound.
A program may use at most 128 MiB of HBM per device.

v0:
```python
import math
import jax
import jax.numpy as jnp
from jax import lax
from jax.sharding import PartitionSpec as P

relaxation = 0.8


def extended(array, sides, width):
    edges = {}
    for axis, dim in sides:
        peers, length = (lax.axis_size(axis), array.shape[dim])
        up = [(i, (i + 1) % peers) for i in range(peers - 1)]
        last = lax.slice_in_dim(array, length - width, length, axis=dim)
        leading = lax.slice_in_dim(array, 0, width, axis=dim)
        edges[dim] = (
            lax.ppermute(last, axis, up),
            lax.ppermute(leading, axis, [(b, a) for a, b in up]),
        )
    done = []
    for _, dim in sides:
        low, high = edges[dim]
        around = [(width, width) if d in done else (0, 0) for d in range(array.ndim)]
        array = jnp.concatenate([jnp.pad(low, around), array, jnp.pad(high, around)], axis=dim)
        done.append(dim)
    return array


def padded_2(array, sides, width):
    for axis, dim in sides:
        peers, length = (lax.axis_size(axis), array.shape[dim])
        up = [(i, (i + 1) % peers) for i in range(peers - 1)]
        down = [(j, i) for i, j in up]
        last = lax.slice_in_dim(array, length - width, length, axis=dim)
        leading = lax.slice_in_dim(array, 0, width, axis=dim)
        before = lax.ppermute(last, axis, up)
        after = lax.ppermute(leading, axis, down)
        array = jnp.concatenate([before, array, after], axis=dim)
    return array


def sent_to_all(array, axis):
    copies = jnp.broadcast_to(array, (lax.axis_size(axis), *array.shape))
    return lax.all_to_all(copies, axis, split_axis=0, concat_axis=0, tiled=True)


def joined_along(tiles, dim):
    tiles = jnp.moveaxis(tiles, 0, dim)
    lengths = tiles.shape
    return tiles.reshape(*lengths[:dim], lengths[dim] * lengths[dim + 1], *lengths[dim + 2 :])


def gathered_copies(array, axis, dim):
    tiles = sent_to_all(array, axis)
    return joined_along(tiles, dim)


def neighbour_sum(padded):
    core = padded[:, :, 1:-1, 1:-1]
    result = padded[:, :, 2:, 1:-1] + padded[:, :, :-2, 1:-1]
    result = result + padded[:, :, 1:-1, 2:] + padded[:, :, 1:-1, :-2]
    zero_layer = jnp.zeros(core.shape[:-1] + (1,), core.dtype)
    upper = jnp.concatenate([core[..., 1:], zero_layer], axis=-1)
    lower = jnp.concatenate([zero_layer, core[..., :-1]], axis=-1)
    return result + upper + lower


def relax_sweep(current, neighbours, source, diagonal_coef, loss_coef):
    real_part = diagonal_coef * current[0] - neighbours[0] - loss_coef * current[1]
    imag_part = diagonal_coef * current[1] - neighbours[1] + loss_coef * current[0]
    applied = jnp.stack([real_part, imag_part])
    return current + relaxation * (source - applied) / diagonal_coef


def block_matrix(radiate):
    upper = jnp.concatenate([radiate[0], radiate[1]], axis=1)
    lower = jnp.concatenate([-radiate[1], radiate[0]], axis=1)
    return jnp.concatenate([upper, lower], axis=0)


def aggregate(leaf_rows, interp, cosine, sine_part):
    parent_count = leaf_rows.shape[0] // 8
    excite = leaf_rows.shape[1]
    spread = jnp.dot(
        leaf_rows.reshape(-1, interp.shape[0]), interp, preferred_element_type=jnp.float32
    )
    spread = spread.reshape(parent_count, 8, excite, 2, interp.shape[1])
    cosine_wide = cosine[None, :, None, :]
    sine_wide = sine_part[None, :, None, :]
    real_part = jnp.sum(cosine_wide * spread[:, :, :, 0] - sine_wide * spread[:, :, :, 1], axis=1)
    imag_part = jnp.sum(sine_wide * spread[:, :, :, 0] + cosine_wide * spread[:, :, :, 1], axis=1)
    return jnp.stack([real_part, imag_part], axis=2).astype(jnp.bfloat16)


def combine_far(sources, table):
    real_table = table[:, :, None, 0]
    imag_table = table[:, :, None, 1]
    real_part = jnp.sum(real_table * sources[:, :, :, 0] - imag_table * sources[:, :, :, 1], axis=1)
    imag_part = jnp.sum(imag_table * sources[:, :, :, 0] + real_table * sources[:, :, :, 1], axis=1)
    return jnp.stack([real_part, imag_part], axis=2)


def disaggregate(incoming_rows, interp, cosine, sine_part, weights):
    parent_count = incoming_rows.shape[0]
    excite = incoming_rows.shape[1]
    widened = incoming_rows.astype(jnp.float32)[:, None]
    cosine_wide = cosine[None, :, None, :]
    sine_wide = sine_part[None, :, None, :]
    real_part = cosine_wide * widened[:, :, :, 0] + sine_wide * widened[:, :, :, 1]
    imag_part = cosine_wide * widened[:, :, :, 1] - sine_wide * widened[:, :, :, 0]
    shifted = jnp.stack([real_part, imag_part], axis=3).astype(jnp.bfloat16)
    leaf_in = jnp.dot(
        shifted.reshape(-1, interp.shape[1]), interp.T, preferred_element_type=jnp.float32
    ).astype(jnp.bfloat16)
    leaf_in = leaf_in.reshape(parent_count * 8 * excite, 2 * interp.shape[0])
    far_part = jnp.dot(leaf_in, weights.T, preferred_element_type=jnp.float32)
    return far_part.reshape(parent_count * 8, excite, weights.shape[0])


def select_cells(flat_field, cell_keys):
    cell_total = flat_field.shape[1]
    block_cells = math.gcd(cell_total, 1024)
    block_total = cell_total // block_cells
    positions = jnp.arange(block_cells, dtype=jnp.int32)

    def add_block(block_index, total):
        first = block_index * block_cells
        piece = lax.dynamic_slice_in_dim(flat_field, first, block_cells, 1)
        selector = (cell_keys[None, :] == (first + positions)[:, None]).astype(jnp.bfloat16)
        return total + jnp.dot(piece, selector, preferred_element_type=jnp.float32)

    empty = jnp.zeros((flat_field.shape[0], cell_keys.shape[0]), jnp.float32)
    return lax.fori_loop(0, block_total, add_block, empty)


def shards(
    volume_field,
    source,
    material,
    mat_real,
    mat_loss,
    surface_map,
    near_boxes,
    near_blocks,
    radiate,
    interp,
    phase_angle,
    far_parents,
    far_kind,
    translate,
):
    excite = volume_field.shape[1]
    cells_x = volume_field.shape[2]
    cells_y = volume_field.shape[3]
    cells_z = volume_field.shape[4]
    diagonal_coef = jnp.full(material.shape, 6.0, jnp.float32)
    loss_coef = jnp.zeros(material.shape, jnp.float32)
    for material_kind in range(mat_real.shape[0]):
        present = material == material_kind
        diagonal_coef = diagonal_coef + jnp.where(present, mat_real[material_kind], 0.0)
        loss_coef = loss_coef + jnp.where(present, mat_loss[material_kind], 0.0)
    current = volume_field
    for sweep_index in range(2):
        padded = extended(current.astype(jnp.bfloat16), (("space", 2), ("shard", 3)), 1).astype(
            current.dtype
        )
        current = relax_sweep(current, neighbour_sum(padded), source, diagonal_coef, loss_coef)
    box_count = surface_map.shape[0]
    unknowns = surface_map.shape[1]
    flat_field = current.reshape(2 * excite, cells_x * cells_y * cells_z).astype(jnp.bfloat16)
    sampled = select_cells(flat_field, surface_map.reshape(-1)).astype(jnp.bfloat16)
    sampled = sampled.reshape(2, excite, box_count, unknowns)
    currents = jnp.transpose(sampled, (2, 1, 0, 3)).reshape(box_count, excite, 2 * unknowns)
    device_rank = lax.axis_index("space") * lax.axis_size("shard") + lax.axis_index("shard")
    beside_all = padded_2(currents, (("shard", 0),), box_count)
    local_near = near_boxes - (device_rank * box_count - box_count)
    near_force = jnp.zeros((box_count, excite, 2 * unknowns), jnp.float32)
    for slot_index in range(near_boxes.shape[1]):
        picked = jnp.take(beside_all, local_near[:, slot_index], axis=0).reshape(
            box_count * excite, 2 * unknowns
        )
        near_force = near_force + jnp.dot(
            picked, near_blocks[slot_index], preferred_element_type=jnp.float32
        ).reshape(box_count, excite, 2 * unknowns)
    weights = block_matrix(radiate)
    leaf_dirs = interp.shape[0]
    leaf = jnp.dot(
        currents.reshape(box_count * excite, 2 * unknowns),
        weights,
        preferred_element_type=jnp.float32,
    ).astype(jnp.bfloat16)
    leaf = leaf.reshape(box_count, excite, 2, leaf_dirs)
    cosine = jnp.cos(phase_angle)
    sine_part = jnp.sin(phase_angle)
    parent_patterns = aggregate(leaf, interp, cosine, sine_part)
    directed = lax.all_to_all(parent_patterns, "shard", split_axis=3, concat_axis=0, tiled=True)
    group_parents = directed.shape[0]
    group_index = lax.axis_index("space")
    target_ids = lax.dynamic_slice_in_dim(
        far_parents, group_index * group_parents, group_parents, 0
    )
    target_kinds = lax.dynamic_slice_in_dim(far_kind, group_index * group_parents, group_parents, 0)
    table = jnp.take(translate, target_kinds, axis=0)
    gathered = gathered_copies(directed, "space", 0)
    sources = jnp.take(gathered, target_ids, axis=0).astype(jnp.float32)
    incoming = combine_far(sources, table).astype(jnp.bfloat16)
    far_force = disaggregate(
        lax.all_to_all(incoming, "shard", split_axis=0, concat_axis=3, tiled=True),
        interp,
        cosine,
        sine_part,
        weights,
    )
    forcing = near_force + far_force
    return (current, forcing)


def solution(mesh):
    return jax.shard_map(
        shards,
        mesh=mesh,
        in_specs=(
            P(None, None, "space", "shard", None),
            P(None, None, "space", "shard", None),
            P("space", "shard", None),
            P(),
            P(),
            P(("space", "shard"), None),
            P(("space", "shard"), None),
            P(),
            P(),
            P(),
            P(),
            P(),
            P(),
            P(None, None, "shard"),
        ),
        out_specs=(P(None, None, "space", "shard", None), P(("space", "shard"), None, None)),
        check_vma=False,
    )
```

profile of v0, /device:TPU:1, one launch (start us, length us, event | category | flops | bytes accessed | tf_op | source)
XLA Modules:
  0.0 238.4 jit_solution(12585446366366786209)
XLA Ops:
  4.2 4.6 %collective-permute-start = (bf16[2,16,4,1,128]{4,3,2,1,0:T(2,128)(2,1)S(1)}, bf16[2,16,4,1,128]{4,3,2,1,0:T(2,128)(2,1)S(1)}, u32[]{:S(2)}, u32[]{:S(2)}) collective-permute-start(bf16[2,16,4,1,128]{4,3,2,1,0:T(2,128)(2,1)S(1)} %get-tuple-element.172), channel_id=1, source_target_pairs={{0,1},{1,2},{2,3},{3,4},{4,5},{5,6},{6,7},{7,8},{8,9},{9,10},{10,1... | collective-permute-start | bytes 98312 | tf_op jit(solution)/shard_map/ppermute | solution.py:18
  8.9 5.0 %collective-permute-start.2 = (bf16[2,16,1,16,128]{4,3,2,1,0:T(8,128)(2,1)S(1)}, bf16[2,16,1,16,128]{4,3,2,1,0:T(8,128)(2,1)S(1)}, u32[]{:S(2)}, u32[]{:S(2)}) collective-permute-start(bf16[2,16,1,16,128]{4,3,2,1,0:T(8,128)(2,1)S(1)} %get-tuple-element.171), channel_id=1, source_target_pairs={{64,0},{128,64},{192,128},{65,1},{129,65},{193,129},{66,2},{130,66... | collective-permute-start | bytes 393224 | tf_op jit(solution)/shard_map/ppermute | solution.py:19
  21.7 5.2 %select_add_fusion.1 = (f32[4,16,128]{2,1,0:T(8,128)S(1)}, pred[4,16,128]{2,1,0:T(8,128)(4,1)S(1)}, pred[4,16,128]{2,1,0:T(8,128)(4,1)S(1)}, pred[4,16,128]{2,1,...) fusion(f32[]{:T(128)} %bitcast.7, f32[]{:T(128)} %bitcast.6, ...), kind=kLoop, calls=%fused_computation.118 | loop fusion | flops 196608 | bytes 131104 | tf_op jit(solution)/shard_map/add | solution.py:161
  26.9 5.0 %select_add_fusion = f32[4,16,128]{2,1,0:T(8,128)S(1)} fusion(pred[4,16,128]{2,1,0:T(8,128)(4,1)S(1)} %get-tuple-element.151, pred[4,16,128]{2,1,0:T(8,128)(4,1)S(1)} %get-tuple-element.150, pred[4,16,128]{2,1,0:T(8,128)(4,1)S(1)} %get-tuple-element.149, pred[4,16,128]{2,1,0:T(8,128)(4,1)S(1)} %get-tuple-element.148, ...), kind=kLoop, calls=%fused_computation.117 | loop fusion | flops 122880 | bytes 98336 | tf_op jit(solution)/shard_map/add | solution.py:162
  38.1 4.6 %collective-permute-start.4 = (bf16[2,16,4,1,128]{4,3,2,1,0:T(2,128)(2,1)}, bf16[2,16,4,1,128]{4,3,2,1,0:T(2,128)(2,1)}, u32[]{:S(2)}, u32[]{:S(2)}) collective-permute-start(bf16[2,16,4,1,128]{4,3,2,1,0:T(2,128)(2,1)} %get-tuple-element.168), channel_id=1, source_target_pairs={{0,1},{1,2},{2,3},{3,4},{4,5},{5,6},{6,7},{7,8},{8,9},{9,10},{10,1... | collective-permute-start | bytes 98312 | tf_op jit(solution)/shard_map/ppermute | solution.py:18
  44.6 5.3 %collective-permute-start.5 = (bf16[2,16,1,16,128]{4,3,2,1,0:T(8,128)(2,1)}, bf16[2,16,1,16,128]{4,3,2,1,0:T(8,128)(2,1)}, u32[]{:S(2)}, u32[]{:S(2)}) collective-permute-start(bf16[2,16,1,16,128]{4,3,2,1,0:T(8,128)(2,1)} %get-tuple-element.166), channel_id=1, source_target_pairs={{0,64},{64,128},{128,192},{1,65},{65,129},{129,193},{2,66},{66,130... | collective-permute-start | bytes 393224 | tf_op jit(solution)/shard_map/ppermute | solution.py:18
  51.8 7.5 %gather_fusion = f32[1024,2,32]{2,1,0:T(2,128)} fusion(f32[316,2,32]{2,1,0:T(2,128)S(1)} %copy.108, s32[1024]{0:T(1024)S(1)} %broadcast_clamp_fusion.1), kind=kCustom, calls=%fused_computation.4 | custom fusion | bytes 528384 | tf_op jit(solution)/shard_map/jit(_take)/gather | solution.py:204
  66.0 12.9 %while.14 = (s32[]{:T(128)}, f32[32,2048]{1,0:T(8,128)S(1)}, bf16[32,8192]{1,0:T(8,128)(2,1)S(1)}, s32[16,128]{1,0:T(8,128)S(1)}, s32[]{:T(128)}, /*index=5*/s32[]{:T(128)}, s32[]{:T(128)}, s32[]{:T(128)}) while((s32[]{:T(128)}, f32[32,2048]{1,0:T(8,128)S(1)}, bf16[32,8192]{1,0:T(8,128)(2,1)S(1)}, s32[16,128]{1,0:T(8,128)S(1)}, ...), condition=%wide.region_1.2_spmd.clone, body=%wide.region_0.1_spmd.clone.sunk | while | flops 136446976 | bytes 606365 | solution.py:134
  83.0 3.7 %copy.113 = bf16[2,16,2,2048]{1,2,0,3:T(2,128)(2,1)} copy(bf16[2,16,2,2048]{3,1,0,2:T(8,128)(2,1)S(1)} %pad_maximum_fusion.2) | data formatting | bytes 524288 | tf_op jit(solution)/shard_map/stack | solution.py:93
  86.6 7.3 %reshape.176 = bf16[64,2,1024]{2,1,0:T(2,128)(2,1)} reshape(bf16[2048,2,2,16]{3,2,1,0:T(2,128)(2,1)} %bitcast.144) | data formatting | bytes 524288
  94.0 16.2 %all-to-all-start = ((bf16[64,2,1024]{2,1,0:T(2,128)(2,1)}), bf16[64,2,1024]{2,1,0:T(2,128)(2,1)S(1)}, u32[]{:S(2)}, u32[]{:S(2)}) async-start(bf16[64,2,1024]{2,1,0:T(2,128)(2,1)} %reshape.176), calls=%async_computation | async-start | bytes 524288 | tf_op jit(solution)/shard_map/all_to_all | solution.py:197
  111.4 9.3 %all-to-all-done = bf16[64,2,1024]{2,1,0:T(2,128)(2,1)S(1)} async-done(((bf16[64,2,1024]{2,1,0:T(2,128)(2,1)}), bf16[64,2,1024]{2,1,0:T(2,128)(2,1)S(1)}, u32[]{:S(2)}, u32[]{:S(2)}) %all-to-all-start) | async-done | bytes 262176 | tf_op jit(solution)/shard_map/all_to_all | solution.py:197
  123.1 5.0 %copy.126 = bf16[2,16,2,64,32]{4,1,2,0,3:T(8,128)(2,1)S(1)} copy(bf16[2,16,2,64,32]{1,2,0,4,3:T(2,128)(2,1)} %bitcast.145) | data formatting | bytes 524288 | tf_op jit(solution)/shard_map/all_to_all | solution.py:197
  139.3 12.0 %collective-permute-done.8 = bf16[16,16,256]{2,1,0:T(8,128)(2,1)S(1)} collective-permute-done((bf16[16,16,256]{2,1,0:T(8,128)(2,1)S(1)}, bf16[16,16,256]{2,1,0:T(8,128)(2,1)S(1)}, u32[]{:S(2)}, u32[]{:S(2)}) %collective-permute-start.8) | collective-permute-done | bytes 131104 | tf_op jit(solution)/shard_map/ppermute | solution.py:37
  155.5 6.4 %copy.117 = bf16[4,128,16,2,32]{4,2,3,1,0:T(8,128)(2,1)} copy(bf16[4,128,16,2,32]{1,4,3,2,0:T(8,128)(2,1)S(1)} %all-to-all-done.1) | data formatting | bytes 2097152 | tf_op jit(solution)/shard_map/all_to_all | solution.py:45
  161.9 12.0 %gather_fusion.1 = bf16[1024,16,2,32]{3,1,2,0:T(8,128)(2,1)} fusion(bf16[512,16,2,32]{3,1,2,0:T(8,128)(2,1)} %bitcast.142, s32[1024]{0:T(1024)S(1)} %broadcast_clamp_fusion), kind=kCustom, calls=%fused_computation.5 | custom fusion | bytes 4198400 | tf_op jit(solution)/shard_map/jit(_take)/gather | solution.py:206
  173.9 5.9 %fusion.11 = f32[128,8,16,2,32]{4,2,1,0,3:T(8,128)S(1)} fusion(bf16[128,8,16,2,32]{4,2,3,1,0:T(8,128)(2,1)} %bitcast.143, pred[128,8]{1,0:T(8,128)(4,1)S(1)} %copy.110), kind=kLoop, calls=%fused_computation.18 | loop fusion | flops 2097152 | bytes 6292480 | tf_op jit(solution)/shard_map/convert_element_type | solution.py:206
  179.9 3.8 %subtract_reduce_fusion = (bf16[128,16,32]{2,1,0:T(8,128)(2,1)S(1)}, bf16[128,16,32]{2,1,0:T(8,128)(2,1)S(1)}) fusion(f32[128,8,16,2,32]{4,2,1,0,3:T(8,128)S(1)} %fusion.11, f32[128,8,32]{2,1,0:T(8,128)S(1)} %copy-done.7, f32[128,8,32]{2,1,0:T(8,128)S(1)} %copy-done.6), kind=kLoop, calls=%fused_computation.20 | loop fusion | flops 4063232 | bytes 4718592 | tf_op jit(solution)/shard_map/reduce_sum | solution.py:99
  187.2 7.5 %all-to-all-start.2 = ((bf16[64,2,1024]{2,1,0:T(2,128)(2,1)}), bf16[64,2,1024]{2,1,0:T(2,128)(2,1)S(1)}, u32[]{:S(2)}, u32[]{:S(2)}) async-start(bf16[64,2,1024]{2,1,0:T(2,128)(2,1)} %reshape.178), calls=%async_computation.2 | async-start | bytes 524288 | tf_op jit(solution)/shard_map/all_to_all | solution.py:209
  209.5 4.2 %copy.123 = f32[2,16,2,64,32]{4,3,1,2,0:T(8,128)} copy(f32[2,16,2,64,32]{4,1,2,0,3:T(8,128)} %bitcast.146) | data formatting | bytes 1048576 | tf_op jit(solution)/shard_map/convert_element_type | solution.py:107
  216.3 4.4 %add_convert_fusion = (bf16[2,8,16,1,2048]{4,3,2,1,0:T(2,128)(2,1)S(1)}, bf16[2,8,16,1,2048]{4,3,2,1,0:T(2,128)(2,1)S(1)}) fusion(f32[2,16,2048]{2,1,0:T(8,128)S(1)} %get-tuple-element.165, f32[8,2048]{1,0:T(8,128)S(1)} %copy-done.13, f32[2,16,2048]{2,1,0:T(8,128)S(1)} %get-tuple-element.164, f32[8,2048]{1,0:T(8,128)S(1)} %copy-done.11), kind=kLoop, calls=%fused_computation.33 | loop fusion | flops 4194304 | bytes 2752512 | tf_op jit(solution)/shard_map/convert.3
  220.7 5.2 %pad_maximum_fusion = bf16[2,8,16,2,2048]{4,3,2,1,0:T(2,128)(2,1)} fusion(bf16[2,8,16,1,2048]{4,3,2,1,0:T(2,128)(2,1)S(1)} %get-tuple-element.163, bf16[2,8,16,1,2048]{4,3,2,1,0:T(2,128)(2,1)S(1)} %get-tuple-element.162), kind=kLoop, calls=%fused_computation.29 | loop fusion | flops 4194304 | bytes 4194304 | tf_op jit(solution)/shard_map/stack | solution.py:112
  225.9 4.1 %convert_element_type.77 = bf16[512,2048]{1,0:T(8,128)(2,1)} reshape(bf16[2,8,16,2,2048]{4,3,2,1,0:T(2,128)(2,1)} %pad_maximum_fusion) | data formatting | bytes 4194304 | tf_op jit(solution)/shard_map/convert_element_type | solution.py:112
  230.0 3.7 %convolution_convert_fusion = bf16[512,512]{1,0:T(8,128)(2,1)} fusion(bf16[512,2048]{1,0:T(8,128)(2,1)} %convert_element_type.77, bf16[512,2048]{1,0:T(8,128)(2,1)S(1)} %copy-done), kind=kOutput, calls=%fused_computation.36 | convolution fusion | flops 1074003968 | bytes 4718592 | tf_op jit(solution)/shard_map/dot_general | solution.py:113
  (155 shorter events, 88.7 us)
Async XLA Ops:
  0.6 80.3 %copy-start = (bf16[512,2048]{1,0:T(8,128)(2,1)S(1)}, bf16[512,2048]{1,0:T(8,128)(2,1)}, u32[]{:S(2)}) copy-start(bf16[512,2048]{1,0:T(8,128)(2,1)} %param.27) | copy-start | bytes 6291460
  0.6 16.3 %copy-start.14 = (bf16[2,128,512]{2,1,0:T(8,128)(2,1)S(1)}, bf16[2,128,512]{2,1,0:T(8,128)(2,1)}, u32[]{:S(2)}) copy-start(bf16[2,128,512]{2,1,0:T(8,128)(2,1)} %param.26) | copy-start | bytes 786436
  0.7 17.7 %copy-start.20 = (f32[8]{0:T(128)S(1)}, f32[8]{0:T(128)}, u32[]{:S(2)}) copy-start(f32[8]{0:T(128)} %param.21) | copy-start | bytes 100
  0.7 18.3 %copy-start.21 = (f32[8]{0:T(128)S(1)}, f32[8]{0:T(128)}, u32[]{:S(2)}) copy-start(f32[8]{0:T(128)} %param.22) | copy-start | bytes 100
  0.7 19.0 %copy-start.19 = (f32[8,2048]{1,0:T(8,128)S(1)}, f32[8,2048]{1,0:T(8,128)}, u32[]{:S(2)}) copy-start(f32[8,2048]{1,0:T(8,128)} %param.28) | copy-start | bytes 196612
  0.7 21.0 %copy-start.22 = (s32[4,16,128]{2,1,0:T(8,128)S(1)}, s32[4,16,128]{2,1,0:T(8,128)}, u32[]{:S(2)}) copy-start(s32[4,16,128]{2,1,0:T(8,128)} %param.20) | copy-start | bytes 98308
  2.9 29.0 %collective-permute-start.3 = (bf16[2,16,4,1,128]{4,3,2,1,0:T(2,128)(2,1)}, bf16[2,16,4,1,128]{4,3,2,1,0:T(2,128)(2,1)S(1)}, u32[]{:S(2)}, u32[]{:S(2)}) collective-permute-start(bf16[2,16,4,1,128]{4,3,2,1,0:T(2,128)(2,1)} %get-tuple-element.173), channel_id=1, source_target_pairs={{1,0},{2,1},{3,2},{4,3},{5,4},{6,5},{7,6},{8,7},{9,8},{10,9},{11,1... | collective-permute-start | bytes 98312 | tf_op jit(solution)/shard_map/ppermute | solution.py:19
  4.2 27.7 %collective-permute-start = (bf16[2,16,4,1,128]{4,3,2,1,0:T(2,128)(2,1)S(1)}, bf16[2,16,4,1,128]{4,3,2,1,0:T(2,128)(2,1)S(1)}, u32[]{:S(2)}, u32[]{:S(2)}) collective-permute-start(bf16[2,16,4,1,128]{4,3,2,1,0:T(2,128)(2,1)S(1)} %get-tuple-element.172), channel_id=1, source_target_pairs={{0,1},{1,2},{2,3},{3,4},{4,5},{5,6},{6,7},{7,8},{8,9},{9,10},{10,1... | collective-permute-start | bytes 98312 | tf_op jit(solution)/shard_map/ppermute | solution.py:18
  8.9 23.1 %collective-permute-start.2 = (bf16[2,16,1,16,128]{4,3,2,1,0:T(8,128)(2,1)S(1)}, bf16[2,16,1,16,128]{4,3,2,1,0:T(8,128)(2,1)S(1)}, u32[]{:S(2)}, u32[]{:S(2)}) collective-permute-start(bf16[2,16,1,16,128]{4,3,2,1,0:T(8,128)(2,1)S(1)} %get-tuple-element.171), channel_id=1, source_target_pairs={{64,0},{128,64},{192,128},{65,1},{129,65},{193,129},{66,2},{130,66... | collective-permute-start | bytes 393224 | tf_op jit(solution)/shard_map/ppermute | solution.py:19
  13.9 18.1 %collective-permute-start.1 = (bf16[2,16,1,16,128]{4,3,2,1,0:T(8,128)(2,1)S(1)}, bf16[2,16,1,16,128]{4,3,2,1,0:T(8,128)(2,1)S(1)}, u32[]{:S(2)}, u32[]{:S(2)}) collective-permute-start(bf16[2,16,1,16,128]{4,3,2,1,0:T(8,128)(2,1)S(1)} %get-tuple-element.170), channel_id=1, source_target_pairs={{0,64},{64,128},{128,192},{1,65},{65,129},{129,193},{2,66},{66,130... | collective-permute-start | bytes 393224 | tf_op jit(solution)/shard_map/ppermute | solution.py:18
  34.9 15.0 %copy-start.23 = (s32[16,4]{0,1:T(4,128)S(1)}, s32[16,4]{0,1:T(4,128)}, u32[]{:S(2)}) copy-start(s32[16,4]{0,1:T(4,128)} %param.24) | copy-start | bytes 772
  36.8 22.5 %collective-permute-start.7 = (bf16[2,16,4,1,128]{4,3,2,1,0:T(2,128)(2,1)}, bf16[2,16,4,1,128]{4,3,2,1,0:T(2,128)(2,1)}, u32[]{:S(2)}, u32[]{:S(2)}) collective-permute-start(bf16[2,16,4,1,128]{4,3,2,1,0:T(2,128)(2,1)} %get-tuple-element.169), channel_id=1, source_target_pairs={{1,0},{2,1},{3,2},{4,3},{5,4},{6,5},{7,6},{8,7},{9,8},{10,9},{11,1... | collective-permute-start | bytes 98312 | tf_op jit(solution)/shard_map/ppermute | solution.py:19
  38.1 21.2 %collective-permute-start.4 = (bf16[2,16,4,1,128]{4,3,2,1,0:T(2,128)(2,1)}, bf16[2,16,4,1,128]{4,3,2,1,0:T(2,128)(2,1)}, u32[]{:S(2)}, u32[]{:S(2)}) collective-permute-start(bf16[2,16,4,1,128]{4,3,2,1,0:T(2,128)(2,1)} %get-tuple-element.168), channel_id=1, source_target_pairs={{0,1},{1,2},{2,3},{3,4},{4,5},{5,6},{6,7},{7,8},{8,9},{9,10},{10,1... | collective-permute-start | bytes 98312 | tf_op jit(solution)/shard_map/ppermute | solution.py:18
  42.7 16.6 %collective-permute-start.6 = (bf16[2,16,1,16,128]{4,3,2,1,0:T(8,128)(2,1)}, bf16[2,16,1,16,128]{4,3,2,1,0:T(8,128)(2,1)}, u32[]{:S(2)}, u32[]{:S(2)}) collective-permute-start(bf16[2,16,1,16,128]{4,3,2,1,0:T(8,128)(2,1)} %get-tuple-element.167), channel_id=1, source_target_pairs={{64,0},{128,64},{192,128},{65,1},{129,65},{193,129},{66,2},{130,66... | collective-permute-start | bytes 393224 | tf_op jit(solution)/shard_map/ppermute | solution.py:19
  44.6 14.7 %collective-permute-start.5 = (bf16[2,16,1,16,128]{4,3,2,1,0:T(8,128)(2,1)}, bf16[2,16,1,16,128]{4,3,2,1,0:T(8,128)(2,1)}, u32[]{:S(2)}, u32[]{:S(2)}) collective-permute-start(bf16[2,16,1,16,128]{4,3,2,1,0:T(8,128)(2,1)} %get-tuple-element.166), channel_id=1, source_target_pairs={{0,64},{64,128},{128,192},{1,65},{65,129},{129,193},{2,66},{66,130... | collective-permute-start | bytes 393224 | tf_op jit(solution)/shard_map/ppermute | solution.py:18
  82.9 27.2 %copy-start.2 = (f32[1024,2,32]{2,1,0:T(2,128)S(1)}, f32[1024,2,32]{2,1,0:T(2,128)}, u32[]{:S(2)}) copy-start(f32[1024,2,32]{2,1,0:T(2,128)} %gather_fusion) | copy-start | bytes 786436
  83.0 27.2 %copy-start.18 = (pred[128,8]{1,0:T(8,128)(4,1)S(1)}, pred[128,8]{1,0:T(8,128)(4,1)}, u32[]{:S(2)}) copy-start(pred[128,8]{1,0:T(8,128)(4,1)} %copy.106) | copy-start | bytes 3076
  94.0 26.8 %all-to-all-start = ((bf16[64,2,1024]{2,1,0:T(2,128)(2,1)}), bf16[64,2,1024]{2,1,0:T(2,128)(2,1)S(1)}, u32[]{:S(2)}, u32[]{:S(2)}) async-start(bf16[64,2,1024]{2,1,0:T(2,128)(2,1)} %reshape.176), calls=%async_computation | async-start | bytes 524288 | tf_op jit(solution)/shard_map/all_to_all | solution.py:197
  130.5 25.0 %all-to-all-start.1 = ((bf16[4,128,16,2,32]{1,4,3,2,0:T(8,128)(2,1)}), bf16[4,128,16,2,32]{1,4,3,2,0:T(8,128)(2,1)S(1)}, u32[]{:S(2)}, u32[]{:S(2)}) async-start(bf16[4,128,16,2,32]{1,4,3,2,0:T(8,128)(2,1)} %broadcast_in_dim.151), calls=%async_computation.1 | async-start | bytes 2097152 | tf_op jit(solution)/shard_map/all_to_all | solution.py:45
  135.0 16.3 %collective-permute-start.8 = (bf16[16,16,256]{2,1,0:T(8,128)(2,1)S(1)}, bf16[16,16,256]{2,1,0:T(8,128)(2,1)S(1)}, u32[]{:S(2)}, u32[]{:S(2)}) collective-permute-start(bf16[16,16,256]{2,1,0:T(8,128)(2,1)S(1)} %reshape.102), channel_id=1, source_target_pairs={{0,1},{1,2},{2,3},{3,4},{4,5},{5,6},{6,7},{7,8},{8,9},{9,10},{10,1... | collective-permute-start | bytes 393224 | tf_op jit(solution)/shard_map/ppermute | solution.py:37
  138.0 14.6 %collective-permute-start.9 = (bf16[16,16,256]{2,1,0:T(8,128)(2,1)S(1)}, bf16[16,16,256]{2,1,0:T(8,128)(2,1)S(1)}, u32[]{:S(2)}, u32[]{:S(2)}) collective-permute-start(bf16[16,16,256]{2,1,0:T(8,128)(2,1)S(1)} %reshape.102), channel_id=1, source_target_pairs={{1,0},{2,1},{3,2},{4,3},{5,4},{6,5},{7,6},{8,7},{9,8},{10,9},{11,1... | collective-permute-start | bytes 393224 | tf_op jit(solution)/shard_map/ppermute | solution.py:38
  173.9 5.9 %copy-start.6 = (f32[128,8,32]{2,1,0:T(8,128)S(1)}, f32[128,8,32]{2,1,0:T(8,128)}, u32[]{:S(2)}) copy-start(f32[128,8,32]{2,1,0:T(8,128)} %get-tuple-element.160) | copy-start | bytes 393220
  173.9 5.9 %copy-start.7 = (f32[128,8,32]{2,1,0:T(8,128)S(1)}, f32[128,8,32]{2,1,0:T(8,128)}, u32[]{:S(2)}) copy-start(f32[128,8,32]{2,1,0:T(8,128)} %get-tuple-element.161) | copy-start | bytes 393220
  187.2 18.4 %all-to-all-start.2 = ((bf16[64,2,1024]{2,1,0:T(2,128)(2,1)}), bf16[64,2,1024]{2,1,0:T(2,128)(2,1)S(1)}, u32[]{:S(2)}, u32[]{:S(2)}) async-start(bf16[64,2,1024]{2,1,0:T(2,128)(2,1)} %reshape.178), calls=%async_computation.2 | async-start | bytes 524288 | tf_op jit(solution)/shard_map/all_to_all | solution.py:209
  (14 other events, 29.6 us)
where the time goes:
time: 240 us; the launch traced here: 238 us
  local copies, waits for them, and re-layouts  89.8 us (37%)
  starting transfers between devices  58.4 us (24%)
  other arithmetic  39.3 us (16%)
  matrix products  27.8 us (12%)
  waiting for transfers between devices  21.3 us (9%)
    ppermute x4, starting transfers between devices, extended(): lax.ppermute(last, axis, up)  17.6 us
    unnamed x58, local copies, waits for them, and re-layouts  16.5 us
    all_to_all x1, starting transfers between devices, shards(): lax.all_to_all(parent_patterns, 'shard', split_axis=3, concat_axis=0, til...  16.2 us
    dot_general x8, matrix products, add_block(): return total + jnp.dot(piece, selector, preferred_element_type=jnp.float32)  12.5 us
    gather x1, local copies, waits for them, and re-layouts, shards(): sources = jnp.take(gathered, target_ids, axis=0).astype(jnp.float32)  12 us
    ppermute x1, waiting for transfers between devices, padded_2(): before = lax.ppermute(last, axis, up)  12 us
    ppermute x4, starting transfers between devices, extended(): lax.ppermute(leading, axis, [(b, a) for a, b in up])  9.48 us
    all_to_all x1, waiting for transfers between devices, shards(): lax.all_to_all(parent_patterns, 'shard', split_axis=3, concat_axis=0, til...  9.3 us
  transfers between devices with their start and end apart: 13, of which 2 were waited for; matrix products, arithmetic and copies ran while one was open for 18% of the time, Pallas kernels for 0%

commit v1 on v0

--- a/solution.py
+++ b/solution.py
@@ -194,7 +194,12 @@
     cosine = jnp.cos(phase_angle)
     sine_part = jnp.sin(phase_angle)
     parent_patterns = aggregate(leaf, interp, cosine, sine_part)
-    directed = lax.all_to_all(parent_patterns, "shard", split_axis=3, concat_axis=0, tiled=True)
+    directed = jnp.concatenate(
+        lax.all_to_all(
+            jnp.stack(jnp.split(parent_patterns, lax.axis_size("shard"), axis=3)), "shard", 0, 0
+        ),
+        axis=0,
+    )
     group_parents = directed.shape[0]
     group_index = lax.axis_index("space")
     target_ids = lax.dynamic_slice_in_dim(

time: 240 us -> 230 us (0.958)
  local copies, waits for them, and re-layouts: 89.8 us -> 75.9 us
  other arithmetic: 39.3 us -> 43.6 us
    all_to_all x2 -> x0, local copies, waits for them, and re-layouts: 6.08 us -> none  [shards(): lax.all_to_all(parent_patterns, 'shard', split_axis=3, concat_axis=0, til...]
    unnamed x58 -> x60, local copies, waits for them, and re-layouts: 16.5 us -> 11.3 us
    unnamed x2 -> x65, other arithmetic: 0.02 us -> 4.28 us
    another operation x1 -> x0, local copies, waits for them, and re-layouts: 3.68 us -> none  [aggregate(): return jnp.stack([real_part, imag_part], axis=2).astype(jnp.bfloat16)]
where the time goes in v1:
time: 230 us; the launch traced here: 229 us
  local copies, waits for them, and re-layouts  75.9 us (33%)
  starting transfers between devices  58.4 us (25%)
  other arithmetic  43.6 us (19%)
  matrix products  27.7 us (12%)
  waiting for transfers between devices  21.3 us (9%)
    ppermute x4, starting transfers between devices, extended(): lax.ppermute(last, axis, up)  17.6 us
    all_to_all x1, starting transfers between devices, shards(): lax.all_to_all(jnp.stack(jnp.split(parent_patterns, lax.axis_size('shard'...  16.2 us
    dot_general x8, matrix products, add_block(): return total + jnp.dot(piece, selector, preferred_element_type=jnp.float32)  12.5 us
    gather x1, local copies, waits for them, and re-layouts, shards(): sources = jnp.take(gathered, target_ids, axis=0).astype(jnp.float32)  12 us
    ppermute x1, waiting for transfers between devices, padded_2(): before = lax.ppermute(last, axis, up)  12 us
    unnamed x60, local copies, waits for them, and re-layouts  11.3 us
    ppermute x4, starting transfers between devices, extended(): lax.ppermute(leading, axis, [(b, a) for a, b in up])  9.48 us
    all_to_all x1, waiting for transfers between devices, shards(): lax.all_to_all(jnp.stack(jnp.split(parent_patterns, lax.axis_size('shard'...  9.29 us
  transfers between devices with their start and end apart: 13, of which 2 were waited for; matrix products, arithmetic and copies ran while one was open for 18% of the time, Pallas kernels for 0%

profile of v1, /device:TPU:1, one launch (start us, length us, event | category | flops | bytes accessed | tf_op | source)
XLA Modules:
  0.0 228.7 jit_solution(321347452824071284)
XLA Ops:
  4.2 4.6 %collective-permute-start = (bf16[2,16,4,1,128]{4,3,2,1,0:T(2,128)(2,1)S(1)}, bf16[2,16,4,1,128]{4,3,2,1,0:T(2,128)(2,1)S(1)}, u32[]{:S(2)}, u32[]{:S(2)}) collective-permute-start(bf16[2,16,4,1,128]{4,3,2,1,0:T(2,128)(2,1)S(1)} %get-tuple-element.172), channel_id=1, source_target_pairs={{0,1},{1,2},{2,3},{3,4},{4,5},{5,6},{6,7},{7,8},{8,9},{9,10},{10,1... | collective-permute-start | bytes 98312 | tf_op jit(solution)/shard_map/ppermute | solution.py:18
  8.9 5.0 %collective-permute-start.2 = (bf16[2,16,1,16,128]{4,3,2,1,0:T(8,128)(2,1)S(1)}, bf16[2,16,1,16,128]{4,3,2,1,0:T(8,128)(2,1)S(1)}, u32[]{:S(2)}, u32[]{:S(2)}) collective-permute-start(bf16[2,16,1,16,128]{4,3,2,1,0:T(8,128)(2,1)S(1)} %get-tuple-element.171), channel_id=1, source_target_pairs={{64,0},{128,64},{192,128},{65,1},{129,65},{193,129},{66,2},{130,66... | collective-permute-start | bytes 393224 | tf_op jit(solution)/shard_map/ppermute | solution.py:19
  13.9 3.0 %collective-permute-start.1 = (bf16[2,16,1,16,128]{4,3,2,1,0:T(8,128)(2,1)S(1)}, bf16[2,16,1,16,128]{4,3,2,1,0:T(8,128)(2,1)S(1)}, u32[]{:S(2)}, u32[]{:S(2)}) collective-permute-start(bf16[2,16,1,16,128]{4,3,2,1,0:T(8,128)(2,1)S(1)} %get-tuple-element.170), channel_id=1, source_target_pairs={{0,64},{64,128},{128,192},{1,65},{65,129},{129,193},{2,66},{66,130... | collective-permute-start | bytes 393224 | tf_op jit(solution)/shard_map/ppermute | solution.py:18
  21.7 5.1 %select_add_fusion.1 = (f32[4,16,128]{2,1,0:T(8,128)S(1)}, pred[4,16,128]{2,1,0:T(8,128)(4,1)S(1)}, pred[4,16,128]{2,1,0:T(8,128)(4,1)S(1)}, pred[4,16,128]{2,1,...) fusion(f32[]{:T(128)} %bitcast.7, f32[]{:T(128)} %bitcast.6, ...), kind=kLoop, calls=%fused_computation.310 | loop fusion | flops 196608 | bytes 131104 | tf_op jit(solution)/shard_map/add | solution.py:161
  26.7 5.0 %select_add_fusion = f32[4,16,128]{2,1,0:T(8,128)S(1)} fusion(pred[4,16,128]{2,1,0:T(8,128)(4,1)S(1)} %get-tuple-element.151, pred[4,16,128]{2,1,0:T(8,128)(4,1)S(1)} %get-tuple-element.150, pred[4,16,128]{2,1,0:T(8,128)(4,1)S(1)} %get-tuple-element.149, pred[4,16,128]{2,1,0:T(8,128)(4,1)S(1)} %get-tuple-element.148, ...), kind=kLoop, calls=%fused_computation.309 | loop fusion | flops 122880 | bytes 98336 | tf_op jit(solution)/shard_map/add | solution.py:162
  37.9 4.6 %collective-permute-start.4 = (bf16[2,16,4,1,128]{4,3,2,1,0:T(2,128)(2,1)}, bf16[2,16,4,1,128]{4,3,2,1,0:T(2,128)(2,1)}, u32[]{:S(2)}, u32[]{:S(2)}) collective-permute-start(bf16[2,16,4,1,128]{4,3,2,1,0:T(2,128)(2,1)} %get-tuple-element.168), channel_id=1, source_target_pairs={{0,1},{1,2},{2,3},{3,4},{4,5},{5,6},{6,7},{7,8},{8,9},{9,10},{10,1... | collective-permute-start | bytes 98312 | tf_op jit(solution)/shard_map/ppermute | solution.py:18
  44.5 5.3 %collective-permute-start.5 = (bf16[2,16,1,16,128]{4,3,2,1,0:T(8,128)(2,1)}, bf16[2,16,1,16,128]{4,3,2,1,0:T(8,128)(2,1)}, u32[]{:S(2)}, u32[]{:S(2)}) collective-permute-start(bf16[2,16,1,16,128]{4,3,2,1,0:T(8,128)(2,1)} %get-tuple-element.166), channel_id=1, source_target_pairs={{0,64},{64,128},{128,192},{1,65},{65,129},{129,193},{2,66},{66,130... | collective-permute-start | bytes 393224 | tf_op jit(solution)/shard_map/ppermute | solution.py:18
  51.6 7.5 %gather_fusion = f32[1024,2,32]{2,1,0:T(2,128)} fusion(f32[316,2,32]{2,1,0:T(2,128)S(1)} %copy.82, s32[1024]{0:T(1024)S(1)} %broadcast_clamp_fusion.1), kind=kCustom, calls=%fused_computation.4 | custom fusion | bytes 528384 | tf_op jit(solution)/shard_map/jit(_take)/gather | solution.py:209
  65.9 12.9 %while.14 = (s32[]{:T(128)}, f32[32,2048]{1,0:T(8,128)S(1)}, bf16[32,8192]{1,0:T(8,128)(2,1)S(1)}, s32[16,128]{1,0:T(8,128)S(1)}, s32[]{:T(128)}, /*index=5*/s32[]{:T(128)}, s32[]{:T(128)}, s32[]{:T(128)}) while((s32[]{:T(128)}, f32[32,2048]{1,0:T(8,128)S(1)}, bf16[32,8192]{1,0:T(8,128)(2,1)S(1)}, s32[16,128]{1,0:T(8,128)S(1)}, ...), condition=%wide.region_1.2_spmd.clone, body=%wide.region_0.1_spmd.clone.sunk | while | flops 136446976 | bytes 606365 | solution.py:134
  88.2 3.1 %reshape.180 = bf16[64,2,1024]{2,1,0:T(2,128)(2,1)} reshape(bf16[64,2,2,16,32]{4,3,2,1,0:T(8,128)(2,1)} %bitcast.402) | data formatting | bytes 524288
  91.3 16.2 %all-to-all-start = ((bf16[64,2,1024]{2,1,0:T(2,128)(2,1)}), bf16[64,2,1024]{2,1,0:T(2,128)(2,1)S(1)}, u32[]{:S(2)}, u32[]{:S(2)}) async-start(bf16[64,2,1024]{2,1,0:T(2,128)(2,1)} %reshape.180), calls=%async_computation | async-start | bytes 524288 | tf_op jit(solution)/shard_map/all_to_all | solution.py:198
  108.7 9.3 %all-to-all-done = bf16[64,2,1024]{2,1,0:T(2,128)(2,1)S(1)} async-done(((bf16[64,2,1024]{2,1,0:T(2,128)(2,1)}), bf16[64,2,1024]{2,1,0:T(2,128)(2,1)S(1)}, u32[]{:S(2)}, u32[]{:S(2)}) %all-to-all-start) | async-done | bytes 262176 | tf_op jit(solution)/shard_map/all_to_all | solution.py:198
  120.9 3.5 %all-to-all-start.1 = ((bf16[4,128,16,2,32]{1,4,3,2,0:T(8,128)(2,1)}), bf16[4,128,16,2,32]{1,4,3,2,0:T(8,128)(2,1)S(1)}, u32[]{:S(2)}, u32[]{:S(2)}) async-start(bf16[4,128,16,2,32]{1,4,3,2,0:T(8,128)(2,1)} %broadcast_in_dim.151), calls=%async_computation.1 | async-start | bytes 2097152 | tf_op jit(solution)/shard_map/all_to_all | solution.py:45
  129.7 12.0 %collective-permute-done.8 = bf16[16,16,256]{2,1,0:T(8,128)(2,1)S(1)} collective-permute-done((bf16[16,16,256]{2,1,0:T(8,128)(2,1)S(1)}, bf16[16,16,256]{2,1,0:T(8,128)(2,1)S(1)}, u32[]{:S(2)}, u32[]{:S(2)}) %collective-permute-start.8) | collective-permute-done | bytes 131104 | tf_op jit(solution)/shard_map/ppermute | solution.py:37
  145.9 6.4 %copy.88 = bf16[4,128,16,2,32]{4,2,3,1,0:T(8,128)(2,1)} copy(bf16[4,128,16,2,32]{1,4,3,2,0:T(8,128)(2,1)S(1)} %all-to-all-done.1) | data formatting | bytes 2097152 | tf_op jit(solution)/shard_map/all_to_all | solution.py:45
  152.3 12.0 %gather_fusion.1 = bf16[1024,16,2,32]{3,1,2,0:T(8,128)(2,1)} fusion(bf16[512,16,2,32]{3,1,2,0:T(8,128)(2,1)} %bitcast.396, s32[1024]{0:T(1024)S(1)} %broadcast_clamp_fusion), kind=kCustom, calls=%fused_computation.5 | custom fusion | bytes 4198400 | tf_op jit(solution)/shard_map/jit(_take)/gather | solution.py:211
  164.3 5.9 %fusion.11 = f32[128,8,16,2,32]{4,2,1,0,3:T(8,128)S(1)} fusion(bf16[128,8,16,2,32]{4,2,3,1,0:T(8,128)(2,1)} %bitcast.397, pred[128,8]{1,0:T(8,128)(4,1)S(1)} %copy.84), kind=kLoop, calls=%fused_computation.18 | loop fusion | flops 2097152 | bytes 6292480 | tf_op jit(solution)/shard_map/convert_element_type | solution.py:211
  170.2 3.8 %subtract_reduce_fusion = (bf16[128,16,32]{2,1,0:T(8,128)(2,1)S(1)}, bf16[128,16,32]{2,1,0:T(8,128)(2,1)S(1)}) fusion(f32[128,8,16,2,32]{4,2,1,0,3:T(8,128)S(1)} %fusion.11, f32[128,8,32]{2,1,0:T(8,128)S(1)} %copy-done.7, f32[128,8,32]{2,1,0:T(8,128)S(1)} %copy-done.6), kind=kLoop, calls=%fused_computation.20 | loop fusion | flops 4063232 | bytes 4718592 | tf_op jit(solution)/shard_map/reduce_sum | solution.py:99
  177.6 7.5 %all-to-all-start.2 = ((bf16[64,2,1024]{2,1,0:T(2,128)(2,1)}), bf16[64,2,1024]{2,1,0:T(2,128)(2,1)S(1)}, u32[]{:S(2)}, u32[]{:S(2)}) async-start(bf16[64,2,1024]{2,1,0:T(2,128)(2,1)} %reshape.182), calls=%async_computation.2 | async-start | bytes 524288 | tf_op jit(solution)/shard_map/all_to_all | solution.py:214
  199.9 4.2 %copy.94 = f32[2,16,2,64,32]{4,3,1,2,0:T(8,128)} copy(f32[2,16,2,64,32]{4,1,2,0,3:T(8,128)} %bitcast.398) | data formatting | bytes 1048576 | tf_op jit(solution)/shard_map/convert_element_type | solution.py:107
  206.7 4.4 %add_convert_fusion = (bf16[2,8,16,1,2048]{4,3,2,1,0:T(2,128)(2,1)S(1)}, bf16[2,8,16,1,2048]{4,3,2,1,0:T(2,128)(2,1)S(1)}) fusion(f32[2,16,2048]{2,1,0:T(8,128)S(1)} %get-tuple-element.165, f32[8,2048]{1,0:T(8,128)S(1)} %copy-done.14, f32[2,16,2048]{2,1,0:T(8,128)S(1)} %get-tuple-element.164, f32[8,2048]{1,0:T(8,128)S(1)} %copy-done.12), kind=kLoop, calls=%fused_computation.159 | loop fusion | flops 4194304 | bytes 2752512 | tf_op jit(solution)/shard_map/convert.3
  211.1 5.2 %pad_maximum_fusion = bf16[2,8,16,2,2048]{4,3,2,1,0:T(2,128)(2,1)} fusion(bf16[2,8,16,1,2048]{4,3,2,1,0:T(2,128)(2,1)S(1)} %get-tuple-element.163, bf16[2,8,16,1,2048]{4,3,2,1,0:T(2,128)(2,1)S(1)} %get-tuple-element.162), kind=kLoop, calls=%fused_computation.155 | loop fusion | flops 4194304 | bytes 4194304 | tf_op jit(solution)/shard_map/stack | solution.py:112
  216.3 4.1 %convert_element_type.77 = bf16[512,2048]{1,0:T(8,128)(2,1)} reshape(bf16[2,8,16,2,2048]{4,3,2,1,0:T(2,128)(2,1)} %pad_maximum_fusion) | data formatting | bytes 4194304 | tf_op jit(solution)/shard_map/convert_element_type | solution.py:112
  220.4 3.7 %convolution_convert_fusion = bf16[512,512]{1,0:T(8,128)(2,1)} fusion(bf16[512,2048]{1,0:T(8,128)(2,1)} %convert_element_type.77, bf16[512,2048]{1,0:T(8,128)(2,1)S(1)} %copy-done), kind=kOutput, calls=%fused_computation.162 | convolution fusion | flops 1074003968 | bytes 4718592 | tf_op jit(solution)/shard_map/dot_general | solution.py:113
  (218 shorter events, 85.5 us)
Async XLA Ops:
  0.6 80.2 %copy-start = (bf16[512,2048]{1,0:T(8,128)(2,1)S(1)}, bf16[512,2048]{1,0:T(8,128)(2,1)}, u32[]{:S(2)}) copy-start(bf16[512,2048]{1,0:T(8,128)(2,1)} %param.27) | copy-start | bytes 6291460
  0.6 16.3 %copy-start.15 = (bf16[2,128,512]{2,1,0:T(8,128)(2,1)S(1)}, bf16[2,128,512]{2,1,0:T(8,128)(2,1)}, u32[]{:S(2)}) copy-start(bf16[2,128,512]{2,1,0:T(8,128)(2,1)} %param.26) | copy-start | bytes 786436
  0.7 17.7 %copy-start.21 = (f32[8]{0:T(128)S(1)}, f32[8]{0:T(128)}, u32[]{:S(2)}) copy-start(f32[8]{0:T(128)} %param.21) | copy-start | bytes 100
  0.7 18.3 %copy-start.22 = (f32[8]{0:T(128)S(1)}, f32[8]{0:T(128)}, u32[]{:S(2)}) copy-start(f32[8]{0:T(128)} %param.22) | copy-start | bytes 100
  0.7 19.0 %copy-start.20 = (f32[8,2048]{1,0:T(8,128)S(1)}, f32[8,2048]{1,0:T(8,128)}, u32[]{:S(2)}) copy-start(f32[8,2048]{1,0:T(8,128)} %param.28) | copy-start | bytes 196612
  0.7 21.0 %copy-start.23 = (s32[4,16,128]{2,1,0:T(8,128)S(1)}, s32[4,16,128]{2,1,0:T(8,128)}, u32[]{:S(2)}) copy-start(s32[4,16,128]{2,1,0:T(8,128)} %param.20) | copy-start | bytes 98308
  2.9 28.9 %collective-permute-start.3 = (bf16[2,16,4,1,128]{4,3,2,1,0:T(2,128)(2,1)}, bf16[2,16,4,1,128]{4,3,2,1,0:T(2,128)(2,1)S(1)}, u32[]{:S(2)}, u32[]{:S(2)}) collective-permute-start(bf16[2,16,4,1,128]{4,3,2,1,0:T(2,128)(2,1)} %get-tuple-element.173), channel_id=1, source_target_pairs={{1,0},{2,1},{3,2},{4,3},{5,4},{6,5},{7,6},{8,7},{9,8},{10,9},{11,1... | collective-permute-start | bytes 98312 | tf_op jit(solution)/shard_map/ppermute | solution.py:19
  4.2 27.6 %collective-permute-start = (bf16[2,16,4,1,128]{4,3,2,1,0:T(2,128)(2,1)S(1)}, bf16[2,16,4,1,128]{4,3,2,1,0:T(2,128)(2,1)S(1)}, u32[]{:S(2)}, u32[]{:S(2)}) collective-permute-start(bf16[2,16,4,1,128]{4,3,2,1,0:T(2,128)(2,1)S(1)} %get-tuple-element.172), channel_id=1, source_target_pairs={{0,1},{1,2},{2,3},{3,4},{4,5},{5,6},{6,7},{7,8},{8,9},{9,10},{10,1... | collective-permute-start | bytes 98312 | tf_op jit(solution)/shard_map/ppermute | solution.py:18
  8.9 22.9 %collective-permute-start.2 = (bf16[2,16,1,16,128]{4,3,2,1,0:T(8,128)(2,1)S(1)}, bf16[2,16,1,16,128]{4,3,2,1,0:T(8,128)(2,1)S(1)}, u32[]{:S(2)}, u32[]{:S(2)}) collective-permute-start(bf16[2,16,1,16,128]{4,3,2,1,0:T(8,128)(2,1)S(1)} %get-tuple-element.171), channel_id=1, source_target_pairs={{64,0},{128,64},{192,128},{65,1},{129,65},{193,129},{66,2},{130,66... | collective-permute-start | bytes 393224 | tf_op jit(solution)/shard_map/ppermute | solution.py:19
  13.9 17.9 %collective-permute-start.1 = (bf16[2,16,1,16,128]{4,3,2,1,0:T(8,128)(2,1)S(1)}, bf16[2,16,1,16,128]{4,3,2,1,0:T(8,128)(2,1)S(1)}, u32[]{:S(2)}, u32[]{:S(2)}) collective-permute-start(bf16[2,16,1,16,128]{4,3,2,1,0:T(8,128)(2,1)S(1)} %get-tuple-element.170), channel_id=1, source_target_pairs={{0,64},{64,128},{128,192},{1,65},{65,129},{129,193},{2,66},{66,130... | collective-permute-start | bytes 393224 | tf_op jit(solution)/shard_map/ppermute | solution.py:18
  34.8 15.0 %copy-start.24 = (s32[16,4]{0,1:T(4,128)S(1)}, s32[16,4]{0,1:T(4,128)}, u32[]{:S(2)}) copy-start(s32[16,4]{0,1:T(4,128)} %param.24) | copy-start | bytes 772
  36.6 22.5 %collective-permute-start.7 = (bf16[2,16,4,1,128]{4,3,2,1,0:T(2,128)(2,1)}, bf16[2,16,4,1,128]{4,3,2,1,0:T(2,128)(2,1)}, u32[]{:S(2)}, u32[]{:S(2)}) collective-permute-start(bf16[2,16,4,1,128]{4,3,2,1,0:T(2,128)(2,1)} %get-tuple-element.169), channel_id=1, source_target_pairs={{1,0},{2,1},{3,2},{4,3},{5,4},{6,5},{7,6},{8,7},{9,8},{10,9},{11,1... | collective-permute-start | bytes 98312 | tf_op jit(solution)/shard_map/ppermute | solution.py:19
  37.9 21.2 %collective-permute-start.4 = (bf16[2,16,4,1,128]{4,3,2,1,0:T(2,128)(2,1)}, bf16[2,16,4,1,128]{4,3,2,1,0:T(2,128)(2,1)}, u32[]{:S(2)}, u32[]{:S(2)}) collective-permute-start(bf16[2,16,4,1,128]{4,3,2,1,0:T(2,128)(2,1)} %get-tuple-element.168), channel_id=1, source_target_pairs={{0,1},{1,2},{2,3},{3,4},{4,5},{5,6},{6,7},{7,8},{8,9},{9,10},{10,1... | collective-permute-start | bytes 98312 | tf_op jit(solution)/shard_map/ppermute | solution.py:18
  42.5 16.6 %collective-permute-start.6 = (bf16[2,16,1,16,128]{4,3,2,1,0:T(8,128)(2,1)}, bf16[2,16,1,16,128]{4,3,2,1,0:T(8,128)(2,1)}, u32[]{:S(2)}, u32[]{:S(2)}) collective-permute-start(bf16[2,16,1,16,128]{4,3,2,1,0:T(8,128)(2,1)} %get-tuple-element.167), channel_id=1, source_target_pairs={{64,0},{128,64},{192,128},{65,1},{129,65},{193,129},{66,2},{130,66... | collective-permute-start | bytes 393224 | tf_op jit(solution)/shard_map/ppermute | solution.py:19
  44.5 14.7 %collective-permute-start.5 = (bf16[2,16,1,16,128]{4,3,2,1,0:T(8,128)(2,1)}, bf16[2,16,1,16,128]{4,3,2,1,0:T(8,128)(2,1)}, u32[]{:S(2)}, u32[]{:S(2)}) collective-permute-start(bf16[2,16,1,16,128]{4,3,2,1,0:T(8,128)(2,1)} %get-tuple-element.166), channel_id=1, source_target_pairs={{0,64},{64,128},{128,192},{1,65},{65,129},{129,193},{2,66},{66,130... | collective-permute-start | bytes 393224 | tf_op jit(solution)/shard_map/ppermute | solution.py:18
  86.5 21.0 %copy-start.2 = (f32[1024,2,32]{2,1,0:T(2,128)S(1)}, f32[1024,2,32]{2,1,0:T(2,128)}, u32[]{:S(2)}) copy-start(f32[1024,2,32]{2,1,0:T(2,128)} %gather_fusion) | copy-start | bytes 786436
  86.5 21.0 %copy-start.19 = (pred[128,8]{1,0:T(8,128)(4,1)S(1)}, pred[128,8]{1,0:T(8,128)(4,1)}, u32[]{:S(2)}) copy-start(pred[128,8]{1,0:T(8,128)(4,1)} %copy.80) | copy-start | bytes 3076
  91.3 26.8 %all-to-all-start = ((bf16[64,2,1024]{2,1,0:T(2,128)(2,1)}), bf16[64,2,1024]{2,1,0:T(2,128)(2,1)S(1)}, u32[]{:S(2)}, u32[]{:S(2)}) async-start(bf16[64,2,1024]{2,1,0:T(2,128)(2,1)} %reshape.180), calls=%async_computation | async-start | bytes 524288 | tf_op jit(solution)/shard_map/all_to_all | solution.py:198
  120.9 25.0 %all-to-all-start.1 = ((bf16[4,128,16,2,32]{1,4,3,2,0:T(8,128)(2,1)}), bf16[4,128,16,2,32]{1,4,3,2,0:T(8,128)(2,1)S(1)}, u32[]{:S(2)}, u32[]{:S(2)}) async-start(bf16[4,128,16,2,32]{1,4,3,2,0:T(8,128)(2,1)} %broadcast_in_dim.151), calls=%async_computation.1 | async-start | bytes 2097152 | tf_op jit(solution)/shard_map/all_to_all | solution.py:45
  125.4 16.3 %collective-permute-start.8 = (bf16[16,16,256]{2,1,0:T(8,128)(2,1)S(1)}, bf16[16,16,256]{2,1,0:T(8,128)(2,1)S(1)}, u32[]{:S(2)}, u32[]{:S(2)}) collective-permute-start(bf16[16,16,256]{2,1,0:T(8,128)(2,1)S(1)} %reshape.105), channel_id=1, source_target_pairs={{0,1},{1,2},{2,3},{3,4},{4,5},{5,6},{6,7},{7,8},{8,9},{9,10},{10,1... | collective-permute-start | bytes 393224 | tf_op jit(solution)/shard_map/ppermute | solution.py:37
  128.4 14.6 %collective-permute-start.9 = (bf16[16,16,256]{2,1,0:T(8,128)(2,1)S(1)}, bf16[16,16,256]{2,1,0:T(8,128)(2,1)S(1)}, u32[]{:S(2)}, u32[]{:S(2)}) collective-permute-start(bf16[16,16,256]{2,1,0:T(8,128)(2,1)S(1)} %reshape.105), channel_id=1, source_target_pairs={{1,0},{2,1},{3,2},{4,3},{5,4},{6,5},{7,6},{8,7},{9,8},{10,9},{11,1... | collective-permute-start | bytes 393224 | tf_op jit(solution)/shard_map/ppermute | solution.py:38
  164.3 5.9 %copy-start.6 = (f32[128,8,32]{2,1,0:T(8,128)S(1)}, f32[128,8,32]{2,1,0:T(8,128)}, u32[]{:S(2)}) copy-start(f32[128,8,32]{2,1,0:T(8,128)} %get-tuple-element.160) | copy-start | bytes 393220
  164.3 5.9 %copy-start.7 = (f32[128,8,32]{2,1,0:T(8,128)S(1)}, f32[128,8,32]{2,1,0:T(8,128)}, u32[]{:S(2)}) copy-start(f32[128,8,32]{2,1,0:T(8,128)} %get-tuple-element.161) | copy-start | bytes 393220
  177.6 18.4 %all-to-all-start.2 = ((bf16[64,2,1024]{2,1,0:T(2,128)(2,1)}), bf16[64,2,1024]{2,1,0:T(2,128)(2,1)S(1)}, u32[]{:S(2)}, u32[]{:S(2)}) async-start(bf16[64,2,1024]{2,1,0:T(2,128)(2,1)} %reshape.182), calls=%async_computation.2 | async-start | bytes 524288 | tf_op jit(solution)/shard_map/all_to_all | solution.py:214
  (15 other events, 30.6 us)
